TPU v7x, 32 devices: a whole 2x2x4 slice. The times are simulated.
32 devices in a mesh: dp: 4 (over y, core), tensor: 2 (over x), pipe: 4 (over z).
Axes of the slice: x: 2, y: 2, z: 4, core: 2. Of those that a mesh axis runs over, the one named last changes fastest.
Arguments:
- grad_parts: float32 [4, 4, 2, 64, 8192], P('dp', 'pipe', 'tensor'), may hold values from -24 to 24
- drop_flags: int32 [4, 4, 2, 64], P('dp', 'pipe', 'tensor'), may hold values from 0 to 1, as said below
- owner_order: int32 [4], replicated, may hold values from 0 to 3, each once
- step_count: int32 [], replicated, may hold values from 1 to 11
- master: float32 [4, 2, 64, 8192], P('pipe', 'tensor', None, 'dp'), may hold values from -6 to 6
- moment_m: float32 [4, 2, 64, 8192], P('pipe', 'tensor', None, 'dp'), may hold values from -0.15625 to 0.15625
- moment_v: float32 [4, 2, 64, 8192], P('pipe', 'tensor', None, 'dp'), may hold values from 0.0001 to 0.001
Outputs:
- new_master: float32 [4, 2, 64, 8192], P('pipe', 'tensor', None, 'dp')
- new_m: float32 [4, 2, 64, 8192], P('pipe', 'tensor', None, 'dp')
- new_v: float32 [4, 2, 64, 8192], P('pipe', 'tensor', None, 'dp')
- direction: float32 [4, 2, 64, 8192], P('pipe', 'tensor', None, 'dp')
- dropped_total: int32 [], replicated
Inputs may be any that keep to these rules, and one draw needn't show every extreme that they name: `drop_flags`: A row may be flagged by every replica.
All inputs are finite; a program needn't handle non-finite values.
Results may differ from a plain program's by a relative error of at most 0.0003.
Values sent between devices are 32-bit elements; how exact they have to be, the bound alone decides.
No kernel may reach another device: no remote copies, remote signals or barrier semaphores. Data moves between devices by JAX's collectives and lax.ppermute only.
A program may use at most 64 MiB of HBM per device.

v0:
```python
import jax
import jax.numpy as jnp
from jax import lax
from jax.sharding import PartitionSpec as P


def body(grad_parts, drop_flags, owner_order, step_count, master, moment_m, moment_v):
    replicas = lax.axis_size("dp")
    flags = drop_flags[0, 0, 0]
    kept = (1 - flags).astype(jnp.float32)
    local_grad = grad_parts[0, 0, 0]
    rows_here = local_grad.shape[0]
    width = local_grad.shape[1]
    block_cols = width // replicas
    term = local_grad * kept[:, None]
    blocks = jnp.take(term.reshape(rows_here, replicas, block_cols), owner_order, axis=1)
    received = lax.all_to_all(blocks, "dp", split_axis=1, concat_axis=1, tiled=True)
    summed = jnp.sum(received, axis=1)
    count = lax.psum(kept, "dp")
    grad = summed / jnp.maximum(count, 1.0)[:, None]
    square_sum, dropped = lax.psum(
        (jnp.sum(grad * grad), jnp.sum(flags).astype(jnp.float32)), ("dp", "tensor", "pipe")
    )
    entries = rows_here * width * lax.axis_size("tensor") * lax.axis_size("pipe")
    rms = jnp.sqrt(square_sum / entries)
    clip = jnp.minimum(1.0, 0.05 / (rms + 1e-06))
    scaled = clip * grad
    old_m = moment_m[0, 0]
    old_v = moment_v[0, 0]
    weights = master[0, 0]
    new_m = 0.9 * old_m + 0.1 * scaled
    new_v = 0.999 * old_v + 0.001 * scaled * scaled
    steps = step_count.astype(jnp.float32)
    m_hat = new_m / (1.0 - jnp.power(0.9, steps))
    v_hat = new_v / (1.0 - jnp.power(0.999, steps))
    direction = m_hat / (jnp.sqrt(v_hat) + 1e-08) + 0.1 * weights
    new_master = weights - 0.001 * direction
    return (
        new_master[None, None],
        new_m[None, None],
        new_v[None, None],
        direction[None, None],
        dropped.astype(jnp.int32),
    )


def solution(mesh):
    return jax.shard_map(
        body,
        mesh=mesh,
        in_specs=(
            P("dp", "pipe", "tensor", None, None),
            P("dp", "pipe", "tensor", None),
            P(),
            P(),
            P("pipe", "tensor", None, "dp"),
            P("pipe", "tensor", None, "dp"),
            P("pipe", "tensor", None, "dp"),
        ),
        out_specs=(
            P("pipe", "tensor", None, "dp"),
            P("pipe", "tensor", None, "dp"),
            P("pipe", "tensor", None, "dp"),
            P("pipe", "tensor", None, "dp"),
            P(),
        ),
        check_vma=False,
    )
```

profile of v0, /device:TPU:0, one launch (start us, length us, event | category | flops | bytes accessed | tf_op | source)
XLA Modules:
  0.0 91.8 jit_solution(3209272403787313384)
XLA Ops:
  0.6 0.7 compare_select_fusion
  1.3 0.7 compare_and_fusion
  2.0 1.3 %fusion.3 = (s32[]{:T(128)}, f32[64]{0:T(128)S(1)}) fusion(s32[1,1,1,64]{3,2,1,0:T(1,128)} %param.8), kind=kLoop, calls=%fused_computation.16 | loop fusion | flops 191 | bytes 516 | tf_op jit(solution)/shard_map/reduce_sum | solution.py:22
  3.2 2.7 %squeeze.2 = f32[64,4,2048]{2,1,0:T(4,128)S(1)} reshape(f32[1,1,1,64,8192]{4,3,2,1,0:T(8,128)} %param.7) | data formatting | bytes 4194304 | tf_op jit(solution)/shard_map/squeeze | solution.py:11
  5.9 2.6 %copy_multiply_fusion = f32[64,4,2048]{2,0,1:T(8,128)} fusion(f32[64,4,2048]{2,1,0:T(4,128)S(1)} %squeeze.2, f32[64]{0:T(128)S(1)} %get-tuple-element.12), kind=kLoop, calls=%fused_computation.1 | loop fusion | flops 524288 | bytes 4194560 | tf_op jit(solution)/shard_map/mul | solution.py:15
  8.5 2.3 %gather_fusion = f32[4,64,2048]{2,1,0:T(8,128)S(1)} fusion(f32[64,4,2048]{2,0,1:T(8,128)} %copy_multiply_fusion, s32[1024]{0:T(1024)S(1)} %pad_clamp_fusion), kind=kCustom, calls=%fused_computation | custom fusion | bytes 4194320 | tf_op jit(solution)/shard_map/jit(_take)/gather | solution.py:16
  10.8 1.6 %select_bitcast_fusion = f32[64,4,2048]{2,0,1:T(8,128)} fusion(f32[4,64,2048]{2,1,0:T(8,128)S(1)} %gather_fusion, pred[4]{0:T(512)(128)(4,1)S(1)} %compare_and_fusion), kind=kLoop, calls=%fused_computation.2 | loop fusion | flops 524288 | bytes 4194308 | tf_op jit(solution)/shard_map/jit(_take)/select_n | solution.py:16
  12.4 4.3 %all-to-all-start = ((f32[64,4,2048]{2,0,1:T(8,128)}), f32[64,4,2048]{2,0,1:T(8,128)S(1)}, u32[]{:S(2)}, u32[]{:S(2)}) async-start(f32[64,4,2048]{2,0,1:T(8,128)} %select_bitcast_fusion), calls=%async_computation | async-start | bytes 4194304 | tf_op jit(solution)/shard_map/all_to_all | solution.py:17
  16.7 0.0 copy-start
  18.1 25.7 %psum.21 = f32[64]{0:T(128)S(1)} all-reduce(f32[64]{0:T(128)S(1)} %get-tuple-element.12), channel_id=1, replica_groups=mesh['dp'=4,'tensor'=2,'pipe'=4] {'dp'}, use_global_device_ids=true, to_apply=%region_1.2 | all-reduce | flops 64 | bytes 512 | tf_op jit(solution)/shard_map/psum | solution.py:19
  43.8 0.0 all-to-all-done
  43.8 0.2 reduce_sum.29
  44.0 0.8 multiply_reduce_fusion
  44.8 41.6 %all-reduce = (f32[]{:T(128)}, f32[]{:T(128)}) all-reduce(f32[]{:T(128)} %multiply_reduce_fusion, f32[]{:T(128)S(6)} %convert_element_type.22), channel_id=1, replica_groups=mesh['dp'=4,'tensor'=2,'pipe'=4] {'dp','tensor','pipe'}, use_global_device_ids=true, to_apply=%region_3.4 | all-reduce | flops 2 | bytes 16 | tf_op jit(solution)/shard_map/psum | solution.py:21
  87.8 0.0 copy-done
  87.8 2.9 %multiply_subtract_fusion = (f32[1,1,64,2048]{3,2,1,0:T(8,128)}, f32[1,1,64,2048]{3,2,1,0:T(8,128)}, f32[1,1,64,2048]{3,2,1,0:T(8,128)}, f32[1,1,64,2048]{3,2,1,0:T(8,128)}) fusion(f32[1,1,64,2048]{3,2,1,0:T(8,128)S(1)} %copy-done, f32[]{:T(128)S(6)} %sub.24, f32[]{:T(128)S(6)} %sub.23, f32[64]{0:T(128)S(1)} %broadcast_maximum_fusion, ...), kind=kLoop, calls=%fused_computation.7 | loop fusion | flops 2228224 | bytes 4194572 | tf_op jit(solution)/shard_map/sub | solution.py:37
  (2 shorter events, 0.0 us)
Async XLA Ops:
  12.4 31.4 %all-to-all-start = ((f32[64,4,2048]{2,0,1:T(8,128)}), f32[64,4,2048]{2,0,1:T(8,128)S(1)}, u32[]{:S(2)}, u32[]{:S(2)}) async-start(f32[64,4,2048]{2,0,1:T(8,128)} %select_bitcast_fusion), calls=%async_computation | async-start | bytes 4194304 | tf_op jit(solution)/shard_map/all_to_all | solution.py:17
  16.7 71.1 %copy-start = (f32[1,1,64,2048]{3,2,1,0:T(8,128)S(1)}, f32[1,1,64,2048]{3,2,1,0:T(8,128)}, u32[]{:S(2)}) copy-start(f32[1,1,64,2048]{3,2,1,0:T(8,128)} %param.11) | copy-start | bytes 1572868
where the time goes:
time: 92.3 us; the launch traced here: 91.8 us
  blocking collectives  67.3 us (73%)
  other arithmetic  10.7 us (12%)
  local copies, waits for them, and re-layouts  4.94 us (5%)
  between operations  4.63 us (5%)
  starting transfers between devices  4.26 us (5%)
    psum x1, blocking collectives, body(): lax.psum((jnp.sum(grad * grad), jnp.sum(flags).astype(jnp.float32)), ('dp...  41.6 us
    psum x1, blocking collectives, body(): count = lax.psum(kept, 'dp')  25.7 us
    all_to_all x1, starting transfers between devices, body(): lax.all_to_all(blocks, 'dp', split_axis=1, concat_axis=1, tiled=True)  4.26 us
    sub x1, other arithmetic, body(): new_master = weights - 0.001 * direction  2.86 us
    squeeze x1, local copies, waits for them, and re-layouts, body(): local_grad = grad_parts[0, 0, 0]  2.67 us
    mul x1, other arithmetic, body(): term = local_grad * kept[:, None]  2.57 us
    select_n x2, other arithmetic, body(): jnp.take(term.reshape(rows_here, replicas, block_cols), owner_order, axis=1)  2.3 us
    gather x1, local copies, waits for them, and re-layouts, body(): jnp.take(term.reshape(rows_here, replicas, block_cols), owner_order, axis=1)  2.27 us
  transfers between devices with their start and end apart: 1, of which 0 were waited for; matrix products, arithmetic and copies ran while one was open for 0% of the time, Pallas kernels for 0%

commit v1 on v0

--- a/solution.py
+++ b/solution.py
@@ -16,7 +16,7 @@
     blocks = jnp.take(term.reshape(rows_here, replicas, block_cols), owner_order, axis=1)
     received = lax.all_to_all(blocks, "dp", split_axis=1, concat_axis=1, tiled=True)
     summed = jnp.sum(received, axis=1)
-    count = lax.psum(kept, "dp")
+    count = jnp.sum(lax.all_gather(kept, "dp"), axis=0)
     grad = summed / jnp.maximum(count, 1.0)[:, None]
     square_sum, dropped = lax.psum(
         (jnp.sum(grad * grad), jnp.sum(flags).astype(jnp.float32)), ("dp", "tensor", "pipe")

time: 92.3 us -> 90.6 us (0.982)
  blocking collectives: 67.3 us -> 65.6 us
    psum x1 -> x0, blocking collectives: 25.7 us -> none  [body(): count = lax.psum(kept, 'dp')]
    all_gather x0 -> x1, blocking collectives: none -> 25.1 us  [body(): count = jnp.sum(lax.all_gather(kept, 'dp'), axis=0)]
    psum x1, blocking collectives: 41.6 us -> 40.5 us  [body(): lax.psum((jnp.sum(grad * grad), jnp.sum(flags).astype(jnp.float32)), ('dp...]
where the time goes in v1:
time: 90.6 us; the launch traced here: 90.2 us
  blocking collectives  65.6 us (72%)
  other arithmetic  10.7 us (12%)
  local copies, waits for them, and re-layouts  4.94 us (5%)
  between operations  4.64 us (5%)
  starting transfers between devices  4.26 us (5%)
    psum x1, blocking collectives, body(): lax.psum((jnp.sum(grad * grad), jnp.sum(flags).astype(jnp.float32)), ('dp...  40.5 us
    all_gather x1, blocking collectives, body(): count = jnp.sum(lax.all_gather(kept, 'dp'), axis=0)  25.1 us
    all_to_all x1, starting transfers between devices, body(): lax.all_to_all(blocks, 'dp', split_axis=1, concat_axis=1, tiled=True)  4.26 us
    sub x1, other arithmetic, body(): new_master = weights - 0.001 * direction  2.86 us
    squeeze x1, local copies, waits for them, and re-layouts, body(): local_grad = grad_parts[0, 0, 0]  2.67 us
    mul x1, other arithmetic, body(): term = local_grad * kept[:, None]  2.57 us
    select_n x2, other arithmetic, body(): jnp.take(term.reshape(rows_here, replicas, block_cols), owner_order, axis=1)  2.3 us
    gather x1, local copies, waits for them, and re-layouts, body(): jnp.take(term.reshape(rows_here, replicas, block_cols), owner_order, axis=1)  2.27 us
  transfers between devices with their start and end apart: 1, of which 0 were waited for; matrix products, arithmetic and copies ran while one was open for 0% of the time, Pallas kernels for 0%

profile of v1, /device:TPU:0, one launch (start us, length us, event | category | flops | bytes accessed | tf_op | source)
XLA Modules:
  0.0 90.2 jit_solution(14291898204369937056)
XLA Ops:
  0.6 0.7 compare_select_fusion
  1.3 0.7 compare_and_fusion
  2.0 1.3 %fusion.4 = (s32[]{:T(128)}, f32[64]{0:T(128)S(1)}, f32[1,1,1,64]{3,2,1,0:T(1,128)S(1)}) fusion(s32[1,1,1,64]{3,2,1,0:T(1,128)} %param.8), kind=kLoop, calls=%fused_computation.17 | loop fusion | flops 191 | bytes 772 | tf_op jit(solution)/shard_map/reduce_sum | solution.py:22
  3.2 2.7 %squeeze.2 = f32[64,4,2048]{2,1,0:T(4,128)S(1)} reshape(f32[1,1,1,64,8192]{4,3,2,1,0:T(8,128)} %param.7) | data formatting | bytes 4194304 | tf_op jit(solution)/shard_map/squeeze | solution.py:11
  5.9 2.6 %copy_multiply_fusion = f32[64,4,2048]{2,0,1:T(8,128)} fusion(f32[64,4,2048]{2,1,0:T(4,128)S(1)} %squeeze.2, f32[64]{0:T(128)S(1)} %get-tuple-element.12), kind=kLoop, calls=%fused_computation.1 | loop fusion | flops 524288 | bytes 4194560 | tf_op jit(solution)/shard_map/mul | solution.py:15
  8.5 2.3 %gather_fusion = f32[4,64,2048]{2,1,0:T(8,128)S(1)} fusion(f32[64,4,2048]{2,0,1:T(8,128)} %copy_multiply_fusion, s32[1024]{0:T(1024)S(1)} %pad_clamp_fusion), kind=kCustom, calls=%fused_computation | custom fusion | bytes 4194320 | tf_op jit(solution)/shard_map/jit(_take)/gather | solution.py:16
  10.8 1.6 %select_bitcast_fusion = f32[64,4,2048]{2,0,1:T(8,128)} fusion(f32[4,64,2048]{2,1,0:T(8,128)S(1)} %gather_fusion, pred[4]{0:T(512)(128)(4,1)S(1)} %compare_and_fusion), kind=kLoop, calls=%fused_computation.2 | loop fusion | flops 524288 | bytes 4194308 | tf_op jit(solution)/shard_map/jit(_take)/select_n | solution.py:16
  12.4 4.3 %all-to-all-start = ((f32[64,4,2048]{2,0,1:T(8,128)}), f32[64,4,2048]{2,0,1:T(8,128)S(1)}, u32[]{:S(2)}, u32[]{:S(2)}) async-start(f32[64,4,2048]{2,0,1:T(8,128)} %select_bitcast_fusion), calls=%async_computation | async-start | bytes 4194304 | tf_op jit(solution)/shard_map/all_to_all | solution.py:17
  16.7 0.0 copy-start
  18.1 25.1 %all-gather = f32[4,1,1,64]{3,2,1,0:T(1,128)S(1)} all-gather(f32[1,1,1,64]{3,2,1,0:T(1,128)S(1)} %get-tuple-element.13), channel_id=2, replica_groups=mesh['dp'=4,'tensor'=2,'pipe'=4] {'dp'}, dimensions={0}, use_global_device_ids=true | all-gather | bytes 1280 | tf_op jit(solution)/shard_map/all_gather | solution.py:19
  43.3 0.0 all-to-all-done
  43.3 0.2 reduce_sum.38
  43.5 0.8 multiply_reduce_fusion
  44.3 40.5 %all-reduce = (f32[]{:T(128)}, f32[]{:T(128)}) all-reduce(f32[]{:T(128)} %multiply_reduce_fusion, f32[]{:T(128)S(6)} %convert_element_type.33), channel_id=1, replica_groups=mesh['dp'=4,'tensor'=2,'pipe'=4] {'dp','tensor','pipe'}, use_global_device_ids=true, to_apply=%region_3.4 | all-reduce | flops 2 | bytes 16 | tf_op jit(solution)/shard_map/psum | solution.py:21
  86.2 0.0 copy-done
  86.2 2.9 %multiply_subtract_fusion = (f32[1,1,64,2048]{3,2,1,0:T(8,128)}, f32[1,1,64,2048]{3,2,1,0:T(8,128)}, f32[1,1,64,2048]{3,2,1,0:T(8,128)}, f32[1,1,64,2048]{3,2,1,0:T(8,128)}) fusion(f32[1,1,64,2048]{3,2,1,0:T(8,128)S(1)} %copy-done, f32[]{:T(128)S(6)} %sub.32, f32[]{:T(128)S(6)} %sub.31, f32[64]{0:T(128)S(1)} %broadcast_maximum_fusion, ...), kind=kLoop, calls=%fused_computation.7 | loop fusion | flops 2228224 | bytes 4194572 | tf_op jit(solution)/shard_map/sub | solution.py:37
  (3 shorter events, 0.0 us)
Async XLA Ops:
  12.4 30.9 %all-to-all-start = ((f32[64,4,2048]{2,0,1:T(8,128)}), f32[64,4,2048]{2,0,1:T(8,128)S(1)}, u32[]{:S(2)}, u32[]{:S(2)}) async-start(f32[64,4,2048]{2,0,1:T(8,128)} %select_bitcast_fusion), calls=%async_computation | async-start | bytes 4194304 | tf_op jit(solution)/shard_map/all_to_all | solution.py:17
  16.7 69.5 %copy-start = (f32[1,1,64,2048]{3,2,1,0:T(8,128)S(1)}, f32[1,1,64,2048]{3,2,1,0:T(8,128)}, u32[]{:S(2)}) copy-start(f32[1,1,64,2048]{3,2,1,0:T(8,128)} %param.11) | copy-start | bytes 1572868
